TPU v7x, 32 devices: a whole 2x2x4 slice. The times are simulated.
32 devices in a mesh: row: 4 (over y, x), blk: 8 (over z, core).
Axes of the slice: x: 2, y: 2, z: 4, core: 2. Of those that a mesh axis runs over, the one named last changes fastest.
Arguments:
- elastic_kernel: bfloat16 [8, 512, 4, 1024], P('blk', None, 'row'), may hold values from -0.125 to 0.125
- slip_deficit: float32 [8, 4, 128, 512], P('blk', 'row'), may hold values from -6 to 6
- state_variable: float32 [8, 4, 128, 512], P('blk', 'row'), may hold values from 0.2 to 5
- step_size: float32 [512], replicated, may hold values from 0.02 to 0.1
- load_stress: float32 [8, 4, 128], P('blk', 'row'), may hold values from -6 to 6
- normal_stress: float32 [8, 4, 128], P('blk', 'row'), may hold values from 0.5 to 2
- rate_table: float32 [16], replicated, may hold values from 0.3 to 1
- evolve_table: float32 [16], replicated, may hold values from 0.3 to 1.5
- patch_region: int32 [8, 4, 128], P('blk', 'row'), may hold values from 0 to 15
- creep_flag: int32 [8, 4, 128], P('blk', 'row'), may hold values 0 or 1
Outputs:
- velocity: float32 [8, 4, 128, 512], P('blk', 'row')
- deficit_out: float32 [8, 4, 128, 512], P('blk', 'row')
- state_out: float32 [8, 4, 128, 512], P('blk', 'row')
- step_next: float32 [512], replicated
All inputs are finite; a program needn't handle non-finite values. Where the computation divides by a largest or mean magnitude, that divisor is 1e-20 or more. No bound on the sum of `creep_flag` on one device may be relied on, other than what follows from the above.
Results may differ from a plain program's by a relative error of at most 0.0035.
Values may be sent and summed in bfloat16 or wider, within the bound.
A program may use at most 64 MiB of HBM per device.

v0:
```python
import jax
import jax.numpy as jnp
from jax import lax
from jax.sharding import PartitionSpec as P

NEWTON = 3
STEPS = 2


DAMPING = 0.5
PLATE_RATE = 1.0
STEP_CAP = 0.5


def inverse_sinh(value):
    magnitude = jnp.abs(value)
    result = jnp.log(magnitude + jnp.sqrt(magnitude * magnitude + 1.0))
    return jnp.where(value < 0.0, -result, result)


def solve_rate(stress, pressure, rate_coef, state_coef, state, creeping):
    factor = 0.5 * jnp.exp(state_coef * jnp.log(state) / rate_coef)
    strength = pressure * rate_coef
    speed = stress / (strength * factor + DAMPING)
    for repeat in range(NEWTON):
        scaled = factor * speed
        mismatch = strength * inverse_sinh(scaled) + DAMPING * speed - stress
        gradient = strength * factor / jnp.sqrt(1.0 + scaled * scaled) + DAMPING
        speed = speed - mismatch / gradient
    return jnp.where(creeping, jnp.float32(PLATE_RATE), speed)


def advance(state, deficit, velocity, step_now):
    new_state = state * jnp.exp(step_now * (1.0 / state - jnp.abs(velocity)))
    new_deficit = deficit + step_now * (velocity - PLATE_RATE)
    return (new_state, new_deficit)


def shards(
    elastic_kernel,
    slip_deficit,
    state_variable,
    step_size,
    load_stress,
    normal_stress,
    rate_table,
    evolve_table,
    patch_region,
    creep_flag,
):
    kernel_tile = elastic_kernel.reshape(elastic_kernel.shape[1], elastic_kernel.shape[3])
    members = slip_deficit.shape[3]
    levels = jnp.arange(rate_table.shape[0], dtype=jnp.int32)
    onehot = (patch_region[..., None] == levels).astype(jnp.float32)
    rate_coef = jnp.sum(onehot * rate_table, axis=-1)[..., None]
    state_coef = jnp.sum(onehot * evolve_table, axis=-1)[..., None]
    pressure = normal_stress[..., None]
    loading = load_stress[..., None]
    creeping = (creep_flag == 1)[..., None]
    deficit = slip_deficit
    state = state_variable
    step_now = step_size
    velocity = jnp.zeros_like(deficit)
    for repeat in range(STEPS):
        slip = deficit.astype(jnp.bfloat16)
        gathered = lax.all_gather(slip, "blk", axis=0, tiled=True)
        sources = gathered.reshape(-1, members)
        owned = lax.psum_scatter(
            jnp.dot(kernel_tile, sources, preferred_element_type=jnp.float32),
            "row",
            scatter_dimension=0,
            tiled=True,
        )
        stress = loading + owned.reshape(slip.shape)
        velocity = solve_rate(stress, pressure, rate_coef, state_coef, state, creeping)
        largest = lax.pmax(jnp.max(jnp.abs(velocity), axis=(0, 1, 2)), ("row", "blk"))
        state, deficit = advance(state, deficit, velocity, step_now)
        step_now = STEP_CAP / (1.0 + largest)
    return (velocity, deficit, state, step_now)


def solution(mesh):
    placed = (
        P("blk", None, "row", None),
        P("blk", "row", None, None),
        P("blk", "row", None, None),
        P(),
        P("blk", "row", None),
        P("blk", "row", None),
        P(),
        P(),
        P("blk", "row", None),
        P("blk", "row", None),
    )
    return jax.shard_map(
        shards,
        mesh=mesh,
        in_specs=placed,
        out_specs=(
            P("blk", "row", None, None),
            P("blk", "row", None, None),
            P("blk", "row", None, None),
            P(),
        ),
        check_vma=False,
    )
```

profile of v0, /device:TPU:0, one launch (start us, length us, event | category | flops | bytes accessed | tf_op | source)
XLA Modules:
  0.0 171.5 jit_solution(2869221156288579903)
XLA Ops:
  7.2 0.0 all-gather.3.cloned.1.call-start
  7.2 1.7 convert_element_type.7
  8.9 0.0 all-gather.3.cloned.1.call-update
  9.0 0.0 reduce-scatter.3.cloned.1.call-start
  9.0 26.2 %all-gather.3.cloned.1.call-done = bf16[8,1,128,512]{3,2,1,0:T(8,128)(2,1)} async-done(((bf16[1,1,128,512]{3,2,1,0:T(8,128)(2,1)}), bf16[8,1,128,512]{3,2,1,0:T(8,128)(2,1)}) %all-gather.3.cloned.1.call-update) | async-done | bytes 1048592 | tf_op jit(solution)/shard_map/all_gather | solution.py:66
  35.2 2.9 %fusion.1 = f32[512,512]{1,0:T(8,128)} fusion(bf16[1024,512]{1,0:T(8,128)(2,1)} %bitcast.43, bf16[1,512,1,1024]{3,1,2,0:T(8,128)(2,1)S(1)} %copy-done), kind=kOutput, calls=%fused_computation.2 | convolution fusion | flops 536870912 | bytes 3145728 | tf_op jit(solution)/shard_map/dot_general | solution.py:69
  38.1 0.0 reduce-scatter.3.cloned.1.call-update
  38.1 0.0 all-gather.5.cloned.1.call-start
  38.2 0.6 copy-done.5
  38.8 0.1 select_reduce_fusion.1
  38.9 0.6 copy-done.9
  39.5 0.7 copy-done.8
  40.1 25.7 %reduce-scatter.3.cloned.1.call-done = f32[128,512]{1,0:T(8,128)} async-done(((f32[512,512]{1,0:T(8,128)}), f32[128,512]{1,0:T(8,128)}) %reduce-scatter.3.cloned.1.call-update) | async-done | bytes 262160 | tf_op jit(solution)/shard_map/reduce_scatter | solution.py:68
  65.8 0.7 copy-done.10
  66.5 2.0 %abs_reduce_fusion.1 = (f32[512]{0:T(512)S(1)}, f32[1,1,128,512]{3,2,1,0:T(8,128)S(1)}) fusion(f32[128]{0:T(128)S(1)} %get-tuple-element.13, f32[128]{0:T(128)S(1)} %get-tuple-element.12, f32[128]{0:T(128)S(1)} %get-tuple-element.5, f32[1,1,128,512]{3,2,1,0:T(8,128)S(1)} %copy-done.2, f32[128]{0:T(128)S(1)} %get-tuple-element.4, ...), kind=kLoop, calls=%fused_computation.51 | loop fusion | flops 3800576 | bytes 791168 | tf_op jit(solution)/shard_map/reduce_max | solution.py:76
  68.5 0.7 fusion.35
  69.2 0.0 reduce-scatter.5.cloned.1.call-start
  69.3 22.3 %all-gather.5.cloned.1.call-done = bf16[8,1,128,512]{3,2,1,0:T(8,128)(2,1)} async-done(((bf16[1,1,128,512]{3,2,1,0:T(8,128)(2,1)}), bf16[8,1,128,512]{3,2,1,0:T(8,128)(2,1)}) %all-gather.5.cloned.1.call-update) | async-done | bytes 1048592 | tf_op jit(solution)/shard_map/all_gather | solution.py:66
  91.6 2.9 %convolution_bitcast_fusion = f32[512,512]{1,0:T(8,128)} fusion(bf16[1024,512]{1,0:T(8,128)(2,1)} %bitcast.44, bf16[1,512,1,1024]{3,1,2,0:T(8,128)(2,1)S(1)} %copy-done), kind=kOutput, calls=%fused_computation | convolution fusion | flops 536870912 | bytes 3145728 | tf_op jit(solution)/shard_map/dot_general | solution.py:69
  94.5 27.6 %reduce-scatter.5.cloned.1.call-done = f32[128,512]{1,0:T(8,128)} async-done(((f32[512,512]{1,0:T(8,128)}), f32[128,512]{1,0:T(8,128)}) %reduce-scatter.5.cloned.1.call-update) | async-done | bytes 262160 | tf_op jit(solution)/shard_map/reduce_scatter | solution.py:68
  122.2 2.0 %abs_reduce_fusion = (f32[512]{0:T(512)S(1)}, f32[1,1,128,512]{3,2,1,0:T(8,128)S(1)}) fusion(f32[128]{0:T(128)S(1)} %get-tuple-element.13, f32[128]{0:T(128)S(1)} %get-tuple-element.12, f32[128]{0:T(128)S(1)} %get-tuple-element.5, f32[1,1,128,512]{3,2,1,0:T(8,128)S(1)} %copy-done.2, f32[1,1,128,512]{3,2,1,0:T(8,128)S(1)} %get-tuple-element.11, ...), kind=kLoop, calls=%fused_computation.50 | loop fusion | flops 4128256 | bytes 1055360 | tf_op jit(solution)/shard_map/reduce_max | solution.py:76
  124.1 39.3 %all-reduce = (f32[512]{0:T(512)S(1)}, f32[512]{0:T(512)S(1)}) all-reduce(f32[512]{0:T(512)S(1)} %get-tuple-element.10, f32[512]{0:T(512)S(1)} %get-tuple-element.8), channel_id=1, replica_groups=mesh['row'=4,'blk'=8] {'row','blk'}, use_global_device_ids=true, to_apply=%region_5.6 | all-reduce | flops 1024 | bytes 8192 | tf_op jit(solution)/shard_map/pmax | solution.py:76
  163.5 0.6 add_divide_fusion
  164.0 1.0 exponential_multiply_fusion
  (22 shorter events, 0.1 us)
Async XLA Ops:
  7.2 28.0 %copy-start = (bf16[1,512,1,1024]{3,1,2,0:T(8,128)(2,1)S(1)}, bf16[1,512,1,1024]{3,1,2,0:T(8,128)(2,1)}, u32[]{:S(2)}) copy-start(bf16[1,512,1,1024]{3,1,2,0:T(8,128)(2,1)} %param.10) | copy-start | bytes 3145732
  7.2 28.0 %all-gather.3.cloned.1.call-start = ((), (), s32[]{:S(2)}) async-start(), calls=%async_computation.2 | async-start | bytes 1179648 | tf_op jit(solution)/shard_map/all_gather | solution.py:66
  9.0 56.8 %reduce-scatter.3.cloned.1.call-start = ((), (), s32[]{:S(2)}) async-start(), calls=%async_computation.3 | async-start | bytes 1310720 | tf_op jit(solution)/shard_map/reduce_scatter | solution.py:68
  38.1 27.8 %copy-start.2 = (f32[1,1,128,512]{3,2,1,0:T(8,128)S(1)}, f32[1,1,128,512]{3,2,1,0:T(8,128)}, u32[]{:S(2)}) copy-start(f32[1,1,128,512]{3,2,1,0:T(8,128)} %param.12) | copy-start | bytes 786436
  38.1 0.7 copy-start.5
  38.1 0.7 copy-start.6
  38.1 0.7 copy-start.7
  38.1 53.5 %all-gather.5.cloned.1.call-start = ((), (), s32[]{:S(2)}) async-start(), calls=%async_computation.4 | async-start | bytes 1179648 | tf_op jit(solution)/shard_map/all_gather | solution.py:66
  38.8 0.7 copy-start.9
  39.5 0.7 copy-start.8
  65.8 0.7 copy-start.10
  66.5 2.0 %copy-start.1 = (f32[1,1,128,512]{3,2,1,0:T(8,128)S(1)}, f32[1,1,128,512]{3,2,1,0:T(8,128)}, u32[]{:S(2)}) copy-start(f32[1,1,128,512]{3,2,1,0:T(8,128)} %param.11) | copy-start | bytes 786436
  66.5 2.0 %copy-start.4 = (f32[512]{0:T(512)S(1)}, f32[512]{0:T(512)}, u32[]{:S(2)}) copy-start(f32[512]{0:T(512)} %param.13) | copy-start | bytes 6148
  69.2 52.9 %reduce-scatter.5.cloned.1.call-start = ((), (), s32[]{:S(2)}) async-start(), calls=%async_computation.5 | async-start | bytes 1310720 | tf_op jit(solution)/shard_map/reduce_scatter | solution.py:68
  124.1 40.9 %copy-start.3 = (f32[1,1,128,512]{3,2,1,0:T(8,128)}, f32[1,1,128,512]{3,2,1,0:T(8,128)S(1)}, u32[]{:S(2)}) copy-start(f32[1,1,128,512]{3,2,1,0:T(8,128)S(1)} %get-tuple-element.9) | copy-start | bytes 786436
Sparse Core Ops, SparseCore 0:
  10.2 24.9 all-gather.2
  38.2 27.5 reduce-scatter.2
  69.3 22.2 all-gather.4
  94.6 27.4 reduce-scatter.4
where the time goes:
time: 172 us
  waiting for transfers between devices  102 us (59%)
  blocking collectives  39.3 us (23%)
  between operations  13.8 us (8%)
  other arithmetic  8.03 us (5%)
  matrix products  5.79 us (3%)
  local copies, waits for them, and re-layouts  2.55 us (1%)
    reduce_scatter x2, waiting for transfers between devices, shards(): lax.psum_scatter(jnp.dot(kernel_tile, sources, preferred_element_type=jnp...  53.3 us
    all_gather x2, waiting for transfers between devices, shards(): gathered = lax.all_gather(slip, 'blk', axis=0, tiled=True)  48.5 us
    pmax x1, blocking collectives, shards(): lax.pmax(jnp.max(jnp.abs(velocity), axis=(0, 1, 2)), ('row', 'blk'))  39.3 us
    dot_general x2, matrix products, shards(): jnp.dot(kernel_tile, sources, preferred_element_type=jnp.float32)  5.79 us
    reduce_max x2, other arithmetic, shards(): jnp.max(jnp.abs(velocity), axis=(0, 1, 2))  3.98 us
  transfers between devices with their start and end apart: 4, of which 4 were waited for; matrix products, arithmetic and copies ran while one was open for 0% of the time, Pallas kernels for 0%

commit v1 on v0

v1 whole, which is shorter than its diff:
```python
import functools

import jax
import jax.numpy as jnp
from jax import lax
from jax.experimental import pallas as pl
from jax.experimental.pallas import tpu as pltpu
from jax.sharding import PartitionSpec as P

NEWTON = 3
STEPS = 2
CORES = 2
CHUNK = 128

DAMPING = 0.5
PLATE_RATE = 1.0
STEP_CAP = 0.5

MESH = pl.DeviceIdType.MESH


def solve_rate(stress, factor, strength, creeping):
    slope = strength * factor
    speed = stress / (slope + DAMPING)
    for repeat in range(NEWTON):
        scaled = factor * speed
        size = jnp.abs(scaled)
        root = jnp.sqrt(size * size + 1.0)
        bend = jnp.log(size + root)
        bend = jnp.where(scaled < 0.0, -bend, bend)
        mismatch = strength * bend + DAMPING * speed - stress
        gradient = slope / root + DAMPING
        speed = speed - mismatch / gradient
    return jnp.where(creeping, jnp.float32(PLATE_RATE), speed)


def fault_kernel(
    rows,
    blks,
    chunks,
    elastic_in,
    deficit_in,
    state_in,
    step_ref,
    load_ref,
    normal_ref,
    rate_ref,
    evolve_ref,
    region_ref,
    creep_ref,
    velocity_out,
    deficit_out,
    state_out,
    next_out,
    tile,
    deficit,
    state,
    velocity,
    gathered,
    parts,
    own,
    partial,
    received,
    coefs,
    max_one,
    max_row,
    max_two,
    max_blk,
    load_sems,
    out_sems,
    own_sems,
    relay_sems,
    slip_sems,
    sum_send,
    sum_recv,
    row_send,
    row_recv,
    blk_send,
    blk_recv,
):
    me_row = lax.axis_index("row")
    me_blk = lax.axis_index("blk")
    spots = blks // CORES
    spot = me_blk // CORES
    core = me_blk % CORES
    elements, width = deficit.shape[1:]
    half = elements // 2
    sent = []

    def columns(c):
        return pl.ds(c * width, width)

    def remote(src, dst, send_sem, recv_sem, row, blk):
        return pltpu.make_async_remote_copy(
            src_ref=src,
            dst_ref=dst,
            send_sem=send_sem,
            recv_sem=recv_sem,
            device_id={"row": row, "blk": blk},
            device_id_type=MESH,
        )

    def launch(copy, when=None):
        if when is None:
            copy.start()
        else:
            pl.when(when)(copy.start)
        sent.append((copy, when))

    deficit_loads = [
        pltpu.make_async_copy(deficit_in.at[:, columns(c)], deficit.at[c], load_sems.at[0, c])
        for c in range(chunks)
    ]
    state_loads = [
        pltpu.make_async_copy(state_in.at[:, columns(c)], state.at[c], load_sems.at[1, c])
        for c in range(chunks)
    ]
    tile_load = pltpu.make_async_copy(elastic_in, tile, load_sems.at[2, 0])
    for copy in deficit_loads + state_loads + [tile_load]:
        copy.start()

    barrier = pltpu.get_barrier_semaphore()
    for j in range(1, rows):
        pl.semaphore_signal(
            barrier,
            inc=1,
            device_id={"row": lax.rem(me_row + j, rows), "blk": me_blk},
            device_id_type=MESH,
        )
    for j in range(1, blks):
        pl.semaphore_signal(
            barrier,
            inc=1,
            device_id={"row": me_row, "blk": lax.rem(me_blk + j, blks)},
            device_id_type=MESH,
        )
    for c in range(chunks):
        deficit_loads[c].wait()
        gathered[0, c, me_blk] = deficit[c].astype(jnp.bfloat16)
    pl.semaphore_wait(barrier, rows + blks - 2)

    def slip_copy(t, c, block, target, sem):
        place = gathered.at[t, c, block]
        return remote(place, place, sem, slip_sems.at[t, c, block], me_row, target)

    def partner_copy(t, c, block, sem):
        return slip_copy(t, c, block, spot * CORES + 1 - core, sem)

    def send_own(t, c):
        for i, shift in enumerate((2, -2, 1, -1)):
            target = spot + shift
            launch(
                slip_copy(t, c, me_blk, target * CORES + core, own_sems.at[t, c, i]),
                (target >= 0) & (target < spots),
            )
        launch(partner_copy(t, c, me_blk, own_sems.at[t, c, 4]))

    def arrived(t, c, block):
        place = gathered.at[t, c, block]
        pltpu.make_async_copy(place, place, slip_sems.at[t, c, block]).wait()

    def gather(t, c):
        order = [d for d in range(1, spots) if d % 2 == 0]
        order += [d for d in range(1, spots) if d % 2 == 1]
        for d in order:
            for i, side in enumerate((-1, 1)):
                source = spot + side * d
                inside = (source >= 0) & (source < spots)
                block = source * CORES + core
                pl.when(inside)(functools.partial(arrived, t, c, block))
                if d % 2 == 0:
                    for j, shift in enumerate((2, 1)):
                        target = spot - side * shift
                        launch(
                            slip_copy(t, c, block, target * CORES + core, relay_sems.at[t, c, d - 1, i, j]),
                            inside & (target >= 0) & (target < spots),
                        )
                launch(partner_copy(t, c, block, relay_sems.at[t, c, d - 1, i, 2]), inside)
        for s in range(spots):
            arrived(t, c, s * CORES + 1 - core)
        total = jnp.dot(
            tile[...],
            gathered[t, c].reshape(blks * elements, width),
            preferred_element_type=jnp.float32,
        ).reshape(rows, elements, width)
        parts[...] = total
        partial[t, c] = total.astype(jnp.bfloat16)
        for j in range(1, rows):
            target = lax.rem(me_row + j, rows)
            launch(
                remote(
                    partial.at[t, c, target],
                    received.at[t, c, j - 1],
                    sum_send.at[t, c, j - 1],
                    sum_recv.at[t, c, j - 1],
                    target,
                    me_blk,
                )
            )
        own[c] = parts[me_row]

    def landed(place, sem):
        pltpu.make_async_copy(place, place, sem).wait()

    def first_round(t, c, largest):
        max_one[t, c] = largest
        for j in range(1, rows):
            launch(
                remote(
                    max_one.at[t, c],
                    max_row.at[t, c, j - 1],
                    row_send.at[t, c, j - 1],
                    row_recv.at[t, c, j - 1],
                    lax.rem(me_row + j, rows),
                    me_blk,
                )
            )

    def second_round(t, c):
        largest = max_one[t, c]
        for j in range(rows - 1):
            landed(max_row.at[t, c, j], row_recv.at[t, c, j])
            largest = jnp.maximum(largest, max_row[t, c, j])
        max_two[t, c] = largest
        for j in range(1, blks):
            launch(
                remote(
                    max_two.at[t, c],
                    max_blk.at[t, c, j - 1],
                    blk_send.at[t, c, j - 1],
                    blk_recv.at[t, c, j - 1],
                    me_row,
                    lax.rem(me_blk + j, blks),
                )
            )

    def next_step(t, c):
        largest = max_two[t, c]
        for j in range(blks - 1):
            landed(max_blk.at[t, c, j], blk_recv.at[t, c, j])
            largest = jnp.maximum(largest, max_blk[t, c, j])
        return STEP_CAP / (1.0 + largest)

    def friction(t, c):
        for h in range(2):
            part = pl.ds(h * half, half)
            coefs[4 + t, c, part] = 0.5 * jnp.exp(jnp.log(state[c, part]) * coefs[2, 0, part])

    def update(t, c):
        for j in range(rows - 1):
            landed(received.at[t, c, j], sum_recv.at[t, c, j])
        last = t == STEPS - 1
        largest = jnp.zeros((1, width), jnp.float32)
        for h in range(2):
            part = pl.ds(h * half, half)
            stress = coefs[0, 0, part] + own[c, part]
            for j in range(rows - 1):
                stress = stress + received[t, c, j, part].astype(jnp.float32)
            speed = solve_rate(stress, coefs[4 + t, c, part], coefs[1, 0, part], coefs[3, 0, part] > 0.5)
            velocity[c, part] = speed
            largest = jnp.maximum(largest, jnp.max(jnp.abs(speed), axis=0, keepdims=True))
            if not last:
                moved = deficit[c, part] + step_ref[:, columns(c)] * (speed - PLATE_RATE)
                deficit[c, part] = moved
                gathered[t + 1, c, me_blk, part] = moved.astype(jnp.bfloat16)
        if last:
            first_round(t, c, largest)
            velocity_stores[c].start()
            step_now = next_step(t - 1, c)
        else:
            send_own(t + 1, c)
            first_round(t, c, largest)
            step_now = step_ref[:, columns(c)]
        for h in range(2):
            part = pl.ds(h * half, half)
            speed = velocity[c, part]
            old = state[c, part]
            state[c, part] = old * jnp.exp(step_now * (1.0 / old - jnp.abs(speed)))
            if last:
                deficit[c, part] = deficit[c, part] + step_now * (speed - PLATE_RATE)
        if last:
            deficit_stores[c].start()
            state_stores[c].start()
        else:
            friction(t + 1, c)

    velocity_stores, deficit_stores, state_stores = (
        [
            pltpu.make_async_copy(held.at[c], out.at[:, columns(c)], out_sems.at[i, c])
            for c in range(chunks)
        ]
        for i, (held, out) in enumerate(
            ((velocity, velocity_out), (deficit, deficit_out), (state, state_out))
        )
    )

    for c in range(chunks):
        send_own(0, c)

    region = region_ref[...]
    rate_coef = jnp.zeros(region.shape, jnp.float32)
    state_coef = jnp.zeros(region.shape, jnp.float32)
    for level in range(rate_ref.shape[0]):
        match = region == level
        rate_coef = jnp.where(match, rate_ref[level], rate_coef)
        state_coef = jnp.where(match, evolve_ref[level], state_coef)

    def spread(line):
        return jnp.transpose(jnp.broadcast_to(line, (width, elements)))

    coefs[0, 0] = spread(load_ref[...])
    coefs[1, 0] = spread(normal_ref[...] * rate_coef)
    coefs[2, 0] = spread(state_coef / rate_coef)
    coefs[3, 0] = spread(jnp.where(creep_ref[...] == 1, 1.0, 0.0))
    for c in range(chunks):
        state_loads[c].wait()
        friction(0, c)
    tile_load.wait()

    stages = [(t, c) for t in range(STEPS) for c in range(chunks)]
    for s in range(len(stages) + 2):
        if s < len(stages):
            gather(*stages[s])
        if 0 <= s - 1 < len(stages):
            update(*stages[s - 1])
        if 0 <= s - 2:
            second_round(*stages[s - 2])
    for c in range(chunks):
        next_out[:, columns(c)] = next_step(STEPS - 1, c)

    for copy in velocity_stores + deficit_stores + state_stores:
        copy.wait()
    for copy, when in sent:
        if when is None:
            copy.wait_send()
        else:
            pl.when(when)(copy.wait_send)


def shards(
    rows,
    blks,
    elastic_kernel,
    slip_deficit,
    state_variable,
    step_size,
    load_stress,
    normal_stress,
    rate_table,
    evolve_table,
    patch_region,
    creep_flag,
):
    elements, members = slip_deficit.shape[2:]
    width = CHUNK if members % CHUNK == 0 else members
    chunks = members // width
    spots = blks // CORES
    anywhere = pl.BlockSpec(memory_space=pl.ANY)
    vmem = pl.BlockSpec(memory_space=pltpu.VMEM)
    smem = pl.BlockSpec(memory_space=pltpu.SMEM)
    block = jax.ShapeDtypeStruct((elements, members), jnp.float32)
    dma = pltpu.SemaphoreType.DMA
    velocity, deficit, state, step_next = pl.pallas_call(
        functools.partial(fault_kernel, rows, blks, chunks),
        out_shape=(block, block, block, jax.ShapeDtypeStruct((1, members), jnp.float32)),
        in_specs=[anywhere] * 3 + [vmem] * 3 + [smem] * 2 + [vmem] * 2,
        out_specs=(anywhere, anywhere, anywhere, vmem),
        scratch_shapes=[
            pltpu.VMEM((elastic_kernel.shape[1], elastic_kernel.shape[3]), jnp.bfloat16),
            pltpu.VMEM((chunks, elements, width), jnp.float32),
            pltpu.VMEM((chunks, elements, width), jnp.float32),
            pltpu.VMEM((chunks, elements, width), jnp.float32),
            pltpu.VMEM((STEPS, chunks, blks, elements, width), jnp.bfloat16),
            pltpu.VMEM((rows, elements, width), jnp.float32),
            pltpu.VMEM((chunks, elements, width), jnp.float32),
            pltpu.VMEM((STEPS, chunks, rows, elements, width), jnp.bfloat16),
            pltpu.VMEM((STEPS, chunks, rows - 1, elements, width), jnp.bfloat16),
            pltpu.VMEM((4 + STEPS, chunks, elements, width), jnp.float32),
            pltpu.VMEM((STEPS, chunks, 1, width), jnp.float32),
            pltpu.VMEM((STEPS, chunks, rows - 1, 1, width), jnp.float32),
            pltpu.VMEM((STEPS, chunks, 1, width), jnp.float32),
            pltpu.VMEM((STEPS, chunks, blks - 1, 1, width), jnp.float32),
            dma((3, chunks)),
            dma((3, chunks)),
            dma((STEPS, chunks, 5)),
            dma((STEPS, chunks, spots - 1, 2, 3)),
            dma((STEPS, chunks, blks)),
            dma((STEPS, chunks, rows - 1)),
            dma((STEPS, chunks, rows - 1)),
            dma((STEPS, chunks, rows - 1)),
            dma((STEPS, chunks, rows - 1)),
            dma((STEPS, chunks, blks - 1)),
            dma((STEPS, chunks, blks - 1)),
        ],
        compiler_params=pltpu.CompilerParams(collective_id=0, has_side_effects=True),
    )(
        elastic_kernel.reshape(elastic_kernel.shape[1], elastic_kernel.shape[3]),
        slip_deficit.reshape(elements, members),
        state_variable.reshape(elements, members),
        step_size.reshape(1, members),
        load_stress.reshape(1, elements),
        normal_stress.reshape(1, elements),
        rate_table,
        evolve_table,
        patch_region.reshape(1, elements),
        creep_flag.reshape(1, elements),
    )
    return (
        velocity.reshape(slip_deficit.shape),
        deficit.reshape(slip_deficit.shape),
        state.reshape(slip_deficit.shape),
        step_next.reshape(members),
    )


def solution(mesh):
    placed = (
        P("blk", None, "row", None),
        P("blk", "row", None, None),
        P("blk", "row", None, None),
        P(),
        P("blk", "row", None),
        P("blk", "row", None),
        P(),
        P(),
        P("blk", "row", None),
        P("blk", "row", None),
    )
    return jax.shard_map(
        functools.partial(shards, mesh.shape["row"], mesh.shape["blk"]),
        mesh=mesh,
        in_specs=placed,
        out_specs=(
            P("blk", "row", None, None),
            P("blk", "row", None, None),
            P("blk", "row", None, None),
            P(),
        ),
        check_vma=False,
    )
```

time: 172 us -> 58.1 us (0.34)
  waiting for transfers between devices: 102 us -> 0 us
  Pallas kernels: 0 us -> 53.2 us
  blocking collectives: 39.3 us -> 0 us
  between operations: 13.8 us -> 0.65 us
  other arithmetic: 8.03 us -> 0 us
  matrix products: 5.79 us -> 0 us
    reduce_scatter x2 -> x0, waiting for transfers between devices: 53.3 us -> none  [shards(): lax.psum_scatter(jnp.dot(kernel_tile, sources, preferred_element_type=jnp...]
    pallas_call x0 -> x1, Pallas kernels: none -> 53.2 us  [shards(): pl.pallas_call(functools.partial(fault_kernel, rows, blks, chunks), out_s...]
    all_gather x2 -> x0, waiting for transfers between devices: 48.5 us -> none  [shards(): gathered = lax.all_gather(slip, 'blk', axis=0, tiled=True)]
    pmax x1 -> x0, blocking collectives: 39.3 us -> none  [shards(): lax.pmax(jnp.max(jnp.abs(velocity), axis=(0, 1, 2)), ('row', 'blk'))]
    dot_general x2 -> x0, matrix products: 5.79 us -> none  [shards(): jnp.dot(kernel_tile, sources, preferred_element_type=jnp.float32)]
    reduce_max x2 -> x0, other arithmetic: 3.98 us -> none  [shards(): jnp.max(jnp.abs(velocity), axis=(0, 1, 2))]
    convert_element_type x2 -> x0, other arithmetic: 2.4 us -> none  [shards(): slip = deficit.astype(jnp.bfloat16)]
    unnamed x22 -> x10, local copies, waits for them, and re-layouts: 2.55 us -> 4.05 us
  transfers between devices with their start and end apart: 4 -> 0, of which waited for: 4 -> 0; matrix products, arithmetic and copies ran while one was open for 0% -> 0% of each run, Pallas kernels for 0% -> 0%
where the time goes in v1:
time: 58.1 us; the launch traced here: 57.9 us
  Pallas kernels  53.2 us (92%)
  local copies, waits for them, and re-layouts  4.05 us (7%)
  between operations  0.65 us (1%)
    pallas_call x1, Pallas kernels, shards(): pl.pallas_call(functools.partial(fault_kernel, rows, blks, chunks), out_s...  53.2 us
    unnamed x10, local copies, waits for them, and re-layouts  4.05 us

profile of v1, /device:TPU:0, one launch (start us, length us, event | category | flops | bytes accessed | tf_op | source)
XLA Modules:
  0.0 57.9 jit_solution(3054703142493744142)
XLA Ops:
  0.6 53.2 %shard_map.129 = (f32[128,512]{1,0:T(8,128)}, f32[128,512]{1,0:T(8,128)}, f32[128,512]{1,0:T(8,128)}, f32[1,512]{1,0:T(1,128)}) custom-call(bf16[512,1024]{1,0:T(8,128)(2,1)} %bitcast.12, f32[128,512]{1,0:T(8,128)} %bitcast.16, f32[128,512]{1,0:T(8,128)} %bitcast.17, f32[1,512]{1,0:T(1,128)} %bitcast.18, f32[1,128]{1,0:T(1,128)} %bitcast.20, ...), custom_call_target="tpu_custom_call" | custom-call | tf_op jit(solution)/shard_map/pallas_call | solution.py:363
  53.9 0.0 copy-start.1
  53.9 1.7 %copy.18 = f32[1,1,128,512]{3,2,1,0:T(8,128)} copy(f32[1,1,128,512]{3,2,1,0:T(8,128)} %bitcast.15) | data formatting | bytes 524288
  55.6 0.0 copy-done.1
  55.6 0.0 copy-start
  55.6 0.7 %copy.19 = f32[1,1,128,512]{3,2,1,0:T(8,128)} copy(f32[1,1,128,512]{3,2,1,0:T(8,128)S(1)} %bitcast.14) | data formatting | bytes 524288
  56.3 0.3 copy-done
  56.6 0.0 copy-start.2
  56.6 0.7 %copy.20 = f32[1,1,128,512]{3,2,1,0:T(8,128)} copy(f32[1,1,128,512]{3,2,1,0:T(8,128)S(1)} %bitcast.13) | data formatting | bytes 524288
  57.3 0.0 copy-done.2
  57.3 0.6 copy.21
Async XLA Ops:
  53.9 1.7 %copy-start.1 = (f32[128,512]{1,0:T(8,128)S(1)}, f32[128,512]{1,0:T(8,128)}, u32[]{:S(2)}) copy-start(f32[128,512]{1,0:T(8,128)} %get-tuple-element.9) | copy-start | bytes 786436
  55.6 1.0 %copy-start = (f32[128,512]{1,0:T(8,128)S(1)}, f32[128,512]{1,0:T(8,128)}, u32[]{:S(2)}) copy-start(f32[128,512]{1,0:T(8,128)} %get-tuple-element.10) | copy-start | bytes 786436
  56.6 0.7 %copy-start.2 = (f32[1,512]{1,0:T(1,128)S(1)}, f32[1,512]{1,0:T(1,128)}, u32[]{:S(2)}) copy-start(f32[1,512]{1,0:T(1,128)} %get-tuple-element.11) | copy-start | bytes 6148

commit v2 on v1

--- a/solution.py
+++ b/solution.py
@@ -11,6 +11,8 @@
 STEPS = 2
 CORES = 2
 CHUNK = 128
+REACH = 2
+EARLY = True
 
 DAMPING = 0.5
 PLATE_RATE = 1.0
@@ -69,8 +71,10 @@
     load_sems,
     out_sems,
     own_sems,
+    partner_sems,
     relay_sems,
     slip_sems,
+    mirror_sems,
     sum_send,
     sum_recv,
     row_send,
@@ -105,7 +109,10 @@
             copy.start()
         else:
             pl.when(when)(copy.start)
-        sent.append((copy, when))
+            sent.append((copy, when))
+
+    def finished(place, sem):
+        pltpu.make_async_copy(place, place, sem).wait()
 
     deficit_loads = [
         pltpu.make_async_copy(deficit_in.at[:, columns(c)], deficit.at[c], load_sems.at[0, c])
@@ -139,45 +146,76 @@
         gathered[0, c, me_blk] = deficit[c].astype(jnp.bfloat16)
     pl.semaphore_wait(barrier, rows + blks - 2)
 
-    def slip_copy(t, c, block, target, sem):
+    reach = min(REACH, spots - 1)
+
+    def slip_copy(t, c, block, target, send_sem, recv_sem):
         place = gathered.at[t, c, block]
-        return remote(place, place, sem, slip_sems.at[t, c, block], me_row, target)
-
-    def partner_copy(t, c, block, sem):
-        return slip_copy(t, c, block, spot * CORES + 1 - core, sem)
+        return remote(place, place, send_sem, recv_sem, me_row, target)
+
+    def mirror(t, c, block, when=None):
+        copy = slip_copy(
+            t,
+            c,
+            block,
+            spot * CORES + 1 - core,
+            partner_sems.at[t, c],
+            mirror_sems.at[t, c],
+        )
+        if when is None:
+            copy.start()
+        else:
+            pl.when(when)(copy.start)
 
     def send_own(t, c):
-        for i, shift in enumerate((2, -2, 1, -1)):
-            target = spot + shift
-            launch(
-                slip_copy(t, c, me_blk, target * CORES + core, own_sems.at[t, c, i]),
-                (target >= 0) & (target < spots),
-            )
-        launch(partner_copy(t, c, me_blk, own_sems.at[t, c, 4]))
-
-    def arrived(t, c, block):
-        place = gathered.at[t, c, block]
-        pltpu.make_async_copy(place, place, slip_sems.at[t, c, block]).wait()
-
-    def gather(t, c):
-        order = [d for d in range(1, spots) if d % 2 == 0]
-        order += [d for d in range(1, spots) if d % 2 == 1]
-        for d in order:
+        for i in range(reach, 0, -1):
+            for j, shift in enumerate((i, -i)):
+                target = spot + shift
+                launch(
+                    slip_copy(
+                        t,
+                        c,
+                        me_blk,
+                        target * CORES + core,
+                        own_sems.at[t, c, i - 1, j],
+                        slip_sems.at[t, c, spot],
+                    ),
+                    (target >= 0) & (target < spots),
+                )
+        mirror(t, c, me_blk)
+
+    def collect(t, c, distances):
+        for d in distances:
             for i, side in enumerate((-1, 1)):
                 source = spot + side * d
                 inside = (source >= 0) & (source < spots)
                 block = source * CORES + core
-                pl.when(inside)(functools.partial(arrived, t, c, block))
-                if d % 2 == 0:
-                    for j, shift in enumerate((2, 1)):
+
+                @pl.when(inside)
+                def _():
+                    finished(gathered.at[t, c, block], slip_sems.at[t, c, source])
+
+                if d % reach == 0:
+                    for shift in range(min(reach, spots - 1 - d), 0, -1):
                         target = spot - side * shift
                         launch(
-                            slip_copy(t, c, block, target * CORES + core, relay_sems.at[t, c, d - 1, i, j]),
+                            slip_copy(
+                                t,
+                                c,
+                                block,
+                                target * CORES + core,
+                                relay_sems.at[t, c, d - 1, i, shift - 1],
+                                slip_sems.at[t, c, source],
+                            ),
                             inside & (target >= 0) & (target < spots),
                         )
-                launch(partner_copy(t, c, block, relay_sems.at[t, c, d - 1, i, 2]), inside)
-        for s in range(spots):
-            arrived(t, c, s * CORES + 1 - core)
+                mirror(t, c, block, inside)
+
+    relayed = [d for d in range(reach, spots, reach) if d < spots - 1]
+    others = [d for d in range(1, spots) if d not in relayed]
+
+    def gather(t, c):
+        collect(t, c, others)
+        finished(gathered.at[t, c, :spots], mirror_sems.at[t, c])
         total = jnp.dot(
             tile[...],
             gathered[t, c].reshape(blks * elements, width),
@@ -191,16 +229,13 @@
                 remote(
                     partial.at[t, c, target],
                     received.at[t, c, j - 1],
-                    sum_send.at[t, c, j - 1],
-                    sum_recv.at[t, c, j - 1],
+                    sum_send.at[t, c],
+                    sum_recv.at[t, c],
                     target,
                     me_blk,
                 )
             )
         own[c] = parts[me_row]
-
-    def landed(place, sem):
-        pltpu.make_async_copy(place, place, sem).wait()
 
     def first_round(t, c, largest):
         max_one[t, c] = largest
@@ -209,8 +244,8 @@
                 remote(
                     max_one.at[t, c],
                     max_row.at[t, c, j - 1],
-                    row_send.at[t, c, j - 1],
-                    row_recv.at[t, c, j - 1],
+                    row_send.at[t, c],
+                    row_recv.at[t, c],
                     lax.rem(me_row + j, rows),
                     me_blk,
                 )
@@ -218,8 +253,8 @@
 
     def second_round(t, c):
         largest = max_one[t, c]
+        finished(max_row.at[t, c], row_recv.at[t, c])
         for j in range(rows - 1):
-            landed(max_row.at[t, c, j], row_recv.at[t, c, j])
             largest = jnp.maximum(largest, max_row[t, c, j])
         max_two[t, c] = largest
         for j in range(1, blks):
@@ -227,8 +262,8 @@
                 remote(
                     max_two.at[t, c],
                     max_blk.at[t, c, j - 1],
-                    blk_send.at[t, c, j - 1],
-                    blk_recv.at[t, c, j - 1],
+                    blk_send.at[t, c],
+                    blk_recv.at[t, c],
                     me_row,
                     lax.rem(me_blk + j, blks),
                 )
@@ -236,8 +271,8 @@
 
     def next_step(t, c):
         largest = max_two[t, c]
+        finished(max_blk.at[t, c], blk_recv.at[t, c])
         for j in range(blks - 1):
-            landed(max_blk.at[t, c, j], blk_recv.at[t, c, j])
             largest = jnp.maximum(largest, max_blk[t, c, j])
         return STEP_CAP / (1.0 + largest)
 
@@ -247,8 +282,7 @@
             coefs[4 + t, c, part] = 0.5 * jnp.exp(jnp.log(state[c, part]) * coefs[2, 0, part])
 
     def update(t, c):
-        for j in range(rows - 1):
-            landed(received.at[t, c, j], sum_recv.at[t, c, j])
+        finished(received.at[t, c], sum_recv.at[t, c])
         last = t == STEPS - 1
         largest = jnp.zeros((1, width), jnp.float32)
         for h in range(2):
@@ -317,24 +351,56 @@
         friction(0, c)
     tile_load.wait()
 
+    def drain(t, c):
+        finished(gathered.at[t, c, :spots], partner_sems.at[t, c])
+        finished(received.at[t, c], sum_send.at[t, c])
+
+    def drain_slips():
+        for copy, when in sent:
+            pl.when(when)(copy.wait_send)
+
+    lag = 1 if chunks > 1 else 0
+    ahead = 1 if EARLY and chunks > 2 else 0
     stages = [(t, c) for t in range(STEPS) for c in range(chunks)]
-    for s in range(len(stages) + 2):
-        if s < len(stages):
+    total = len(stages)
+    for s in range(ahead):
+        collect(*stages[s], relayed)
+    for s in range(total + lag + 1):
+        if not ahead and s < total:
+            collect(*stages[s], relayed)
+        if s < total:
             gather(*stages[s])
-        if 0 <= s - 1 < len(stages):
-            update(*stages[s - 1])
-        if 0 <= s - 2:
-            second_round(*stages[s - 2])
+        if ahead and s + ahead < total:
+            collect(*stages[s + ahead], relayed)
+        if 0 <= s - lag < total:
+            update(*stages[s - lag])
+        if s == total + lag - 1:
+            for stage in stages:
+                drain(*stage)
+            drain_slips()
+        if 0 <= s - lag - 1 < total:
+            second_round(*stages[s - lag - 1])
+    for copy in velocity_stores + deficit_stores + state_stores:
+        copy.wait()
+    for t, c in stages:
+        finished(max_row.at[t, c], row_send.at[t, c])
+        finished(max_blk.at[t, c], blk_send.at[t, c])
     for c in range(chunks):
         next_out[:, columns(c)] = next_step(STEPS - 1, c)
 
-    for copy in velocity_stores + deficit_stores + state_stores:
+
+def hand_over(velocity_in, deficit_in, state_in, next_in, velocity_out, deficit_out, state_out, next_out, held, sems):
+    pairs = ((velocity_in, velocity_out), (deficit_in, deficit_out), (state_in, state_out))
+    loads = [pltpu.make_async_copy(pair[0], held.at[i], sems.at[0, i]) for i, pair in enumerate(pairs)]
+    stores = [pltpu.make_async_copy(held.at[i], pair[1], sems.at[1, i]) for i, pair in enumerate(pairs)]
+    for copy in loads:
+        copy.start()
+    next_out[...] = next_in[...]
+    for load, store in zip(loads, stores):
+        load.wait()
+        store.start()
+    for copy in stores:
         copy.wait()
-    for copy, when in sent:
-        if when is None:
-            copy.wait_send()
-        else:
-            pl.when(when)(copy.wait_send)
 
 
 def shards(
@@ -355,12 +421,13 @@
     width = CHUNK if members % CHUNK == 0 else members
     chunks = members // width
     spots = blks // CORES
+    reach = min(REACH, spots - 1)
     anywhere = pl.BlockSpec(memory_space=pl.ANY)
     vmem = pl.BlockSpec(memory_space=pltpu.VMEM)
     smem = pl.BlockSpec(memory_space=pltpu.SMEM)
     block = jax.ShapeDtypeStruct((elements, members), jnp.float32)
     dma = pltpu.SemaphoreType.DMA
-    velocity, deficit, state, step_next = pl.pallas_call(
+    solved = pl.pallas_call(
         functools.partial(fault_kernel, rows, blks, chunks),
         out_shape=(block, block, block, jax.ShapeDtypeStruct((1, members), jnp.float32)),
         in_specs=[anywhere] * 3 + [vmem] * 3 + [smem] * 2 + [vmem] * 2,
@@ -382,15 +449,17 @@
             pltpu.VMEM((STEPS, chunks, blks - 1, 1, width), jnp.float32),
             dma((3, chunks)),
             dma((3, chunks)),
-            dma((STEPS, chunks, 5)),
-            dma((STEPS, chunks, spots - 1, 2, 3)),
-            dma((STEPS, chunks, blks)),
-            dma((STEPS, chunks, rows - 1)),
-            dma((STEPS, chunks, rows - 1)),
-            dma((STEPS, chunks, rows - 1)),
-            dma((STEPS, chunks, rows - 1)),
-            dma((STEPS, chunks, blks - 1)),
-            dma((STEPS, chunks, blks - 1)),
+            dma((STEPS, chunks, reach, 2)),
+            dma((STEPS, chunks)),
+            dma((STEPS, chunks, spots - 1, 2, reach)),
+            dma((STEPS, chunks, spots)),
+            dma((STEPS, chunks)),
+            dma((STEPS, chunks)),
+            dma((STEPS, chunks)),
+            dma((STEPS, chunks)),
+            dma((STEPS, chunks)),
+            dma((STEPS, chunks)),
+            dma((STEPS, chunks)),
         ],
         compiler_params=pltpu.CompilerParams(collective_id=0, has_side_effects=True),
     )(
@@ -405,6 +474,13 @@
         patch_region.reshape(1, elements),
         creep_flag.reshape(1, elements),
     )
+    velocity, deficit, state, step_next = pl.pallas_call(
+        hand_over,
+        out_shape=(block, block, block, jax.ShapeDtypeStruct((1, members), jnp.float32)),
+        in_specs=[anywhere] * 3 + [vmem],
+        out_specs=(anywhere, anywhere, anywhere, vmem),
+        scratch_shapes=[pltpu.VMEM((3, elements, members), jnp.float32), dma((2, 3))],
+    )(*solved)
     return (
         velocity.reshape(slip_deficit.shape),
         deficit.reshape(slip_deficit.shape),

time: 58.1 us -> 52.7 us (0.907)
  local copies, waits for them, and re-layouts: 4.05 us -> 0 us
  Pallas kernels: 53.2 us -> 51.8 us
    pallas_call x1, Pallas kernels: 53.2 us -> 48.7 us  [shards(): pl.pallas_call(functools.partial(fault_kernel, rows, blks, chunks), out_s...]
    unnamed x10 -> x0, local copies, waits for them, and re-layouts: 4.05 us -> none
    pallas_call x0 -> x1, Pallas kernels: none -> 3.11 us  [shards(): pl.pallas_call(hand_over, out_shape=(block, block, block, jax.ShapeDtypeS...]
where the time goes in v2:
time: 52.7 us; the launch traced here: 52.5 us
  Pallas kernels  51.8 us (98%)
  between operations  0.64 us (1%)
    pallas_call x1, Pallas kernels, shards(): pl.pallas_call(functools.partial(fault_kernel, rows, blks, chunks), out_s...  48.7 us
    pallas_call x1, Pallas kernels, shards(): pl.pallas_call(hand_over, out_shape=(block, block, block, jax.ShapeDtypeS...  3.11 us

profile of v2, /device:TPU:0, one launch (start us, length us, event | category | flops | bytes accessed | tf_op | source)
XLA Modules:
  0.0 52.5 jit_solution(1519640310767464268)
XLA Ops:
  0.6 48.7 %shard_map.129 = (f32[128,512]{1,0:T(8,128)}, f32[128,512]{1,0:T(8,128)}, f32[128,512]{1,0:T(8,128)}, f32[1,512]{1,0:T(1,128)}) custom-call(bf16[512,1024]{1,0:T(8,128)(2,1)} %bitcast.12, f32[128,512]{1,0:T(8,128)} %bitcast.13, f32[128,512]{1,0:T(8,128)} %bitcast.14, f32[1,512]{1,0:T(1,128)} %bitcast.15, f32[1,128]{1,0:T(1,128)} %bitcast.16, ...), custom_call_target="tpu_custom_call" | custom-call | tf_op jit(solution)/shard_map/pallas_call | solution.py:430
  49.4 3.1 %shard_map.130 = (f32[128,512]{1,0:T(8,128)}, f32[128,512]{1,0:T(8,128)}, f32[128,512]{1,0:T(8,128)}, f32[1,512]{1,0:T(1,128)}) custom-call(f32[128,512]{1,0:T(8,128)} %get-tuple-element.12.velocity_in, f32[128,512]{1,0:T(8,128)} %get-tuple-element.13.deficit_in, f32[128,512]{1,0:T(8,128)} %get-tuple-element.14.state_in, f32[1,512]{1,0:T(1,128)} %get-tuple-element.15.next_in), custom_call_target="tpu_custom_call" | custom-call | tf_op jit(solution)/shard_map/pallas_call | solution.py:477
